TPU v7x, 256 devices: a whole 4x4x8 slice. The times are simulated.
256 devices in a mesh: dp: 16 (over x, z_hi, core), seq: 16 (over z_lo, y).
Axes of the slice: x: 4, y: 4, z: 8 (z_hi: 2, z_lo: 4; z = z_hi * 4 + z_lo), core: 2. Of those that a mesh axis runs over, the one named last changes fastest.
Arguments:
- tokens: bfloat16 [32, 2304, 1280], P('dp', 'seq'), may hold values from -60 to 60
- pre_gain: float32 [1280], replicated, may hold values from 0.5 to 1.5
- pre_shift: float32 [1280], replicated, may hold values from -3 to 3
- w_qkv: bfloat16 [1280, 3840], P('dp'), may hold values from -4 to 4
- qkv_bias: float32 [3840], replicated, may hold values from -3 to 3
- w_out: bfloat16 [1280, 1280], P('dp'), may hold values from -0.15625 to 0.15625
- out_bias: float32 [1280], replicated, may hold values from -3 to 3
- mlp_gain: float32 [1280], replicated, may hold values from 0.5 to 1.5
- mlp_shift: float32 [1280], replicated, may hold values from -3 to 3
- w_up: bfloat16 [1280, 2560], P('dp'), may hold values from -0.15625 to 0.15625
- up_bias: float32 [2560], replicated, may hold values from -3 to 3
- w_down: bfloat16 [2560, 1280], P('dp'), may hold values from -0.125 to 0.125
- down_bias: float32 [1280], replicated, may hold values from -3 to 3
Outputs:
- layer_out: bfloat16 [32, 2304, 1280], P('dp', 'seq')
All inputs are finite; a program needn't handle non-finite values.
Results may differ from a plain program's by a relative error of at most 0.0039.
Values may be sent and summed in bfloat16 or wider, within the bound.
A program may use at most 128 MiB of HBM per device.

v0:
```python
import math
import jax
import jax.numpy as jnp
from jax import lax
from jax.sharding import PartitionSpec as P

HEADS = 16
HEAD_DIM = 80
EPSILON = 1e-05


def grouped_exchange(array, axis, split_dim, concat_dim, work, item_dim, out_dim):

    def moved(group):
        return lax.all_to_all(group, axis, split_axis=split_dim, concat_axis=concat_dim, tiled=True)

    items = jax.tree.leaves(array)[0].shape[item_dim]
    ends = [items * k // 2 for k in range(2 + 1)] if items % 2 == 0 else [0, items]
    groups = [
        jax.tree.map(lambda a: lax.slice_in_dim(a, low, high, axis=item_dim), array)
        for low, high in zip(ends, ends[1:])
    ]
    arrived = [moved(group) for group in groups]
    made = [work(group) for group in arrived]
    return jax.tree.map(lambda *parts: jnp.concatenate(parts, axis=out_dim), *made)


def normalize(features, gain, shift):
    average = jnp.mean(features, axis=-1, keepdims=True)
    centered = features - average
    spread = jnp.mean(centered * centered, axis=-1, keepdims=True)
    return centered * lax.rsqrt(spread + EPSILON) * gain + shift


def fold_rows(left_side, shard_piece):
    return jnp.dot(left_side, shard_piece, preferred_element_type=jnp.float32)


def query_block(length):
    block_rows = length
    while block_rows > 1024 and block_rows % 2 == 0:
        block_rows = block_rows // 2
    return block_rows


def attend_back(packed_items):
    count, length, heads_here, triple = packed_items.shape
    head_size = triple // 3
    block_rows = query_block(length)
    factor = 1.0 / math.sqrt(head_size)

    def one_picture(picture):
        key_rows = picture[:, :, head_size : 2 * head_size]
        value_rows = picture[:, :, 2 * head_size :]
        queries = picture[:, :, :head_size].reshape(
            length // block_rows, block_rows, heads_here, head_size
        )

        def one_block(query_rows):
            scores = (
                jnp.einsum("qhd,khd->hqk", query_rows, key_rows, preferred_element_type=jnp.float32)
                * factor
            )
            highest = jnp.max(scores, axis=-1, keepdims=True)
            weights = jnp.exp(scores - highest)
            probs = (weights / jnp.sum(weights, axis=-1, keepdims=True)).astype(jnp.bfloat16)
            mixed = jnp.einsum(
                "hqk,khd->qhd", probs, value_rows, preferred_element_type=jnp.float32
            )
            return mixed.astype(jnp.bfloat16)

        outputs = lax.map(one_block, queries)
        return outputs.reshape(length, heads_here * head_size)

    context = lax.map(one_picture, packed_items)
    return lax.all_to_all(context, "seq", split_axis=1, concat_axis=2, tiled=True)


def shards(
    tokens,
    pre_gain,
    pre_shift,
    w_qkv,
    qkv_bias,
    w_out,
    out_bias,
    mlp_gain,
    mlp_shift,
    w_up,
    up_bias,
    w_down,
    down_bias,
):
    images_here, tok_here, width = tokens.shape
    row_count = images_here * tok_here
    triple = 3 * HEAD_DIM
    residual = tokens.reshape(row_count, width).astype(jnp.float32)
    normed = normalize(residual, pre_gain, pre_shift).astype(jnp.bfloat16)
    projected = fold_rows(normed, lax.all_gather(w_qkv, "dp", axis=0, tiled=True))
    packed = (
        (projected + qkv_bias).astype(jnp.bfloat16).reshape(images_here, tok_here, HEADS, triple)
    )
    context = grouped_exchange(packed, "seq", 2, 1, attend_back, 0, 0)
    context = context.reshape(row_count, width)
    attended = fold_rows(context, lax.all_gather(w_out, "dp", axis=0, tiled=True))
    middle = residual + attended + out_bias
    normed_mlp = normalize(middle, mlp_gain, mlp_shift).astype(jnp.bfloat16)
    lifted = fold_rows(normed_mlp, lax.all_gather(w_up, "dp", axis=0, tiled=True))
    hidden = jax.nn.gelu(lifted + up_bias, approximate=False).astype(jnp.bfloat16)
    lowered = fold_rows(hidden, lax.all_gather(w_down, "dp", axis=0, tiled=True))
    result = (middle + lowered + down_bias).astype(jnp.bfloat16)
    return result.reshape(images_here, tok_here, width)


def solution(mesh):
    in_specs = (
        P("dp", "seq", None),
        P(),
        P(),
        P("dp", None),
        P(),
        P("dp", None),
        P(),
        P(),
        P(),
        P("dp", None),
        P(),
        P("dp", None),
        P(),
    )
    out_specs = P("dp", "seq", None)
    return jax.shard_map(shards, mesh=mesh, in_specs=in_specs, out_specs=out_specs, check_vma=False)
```

profile of v0, /device:TPU:1, one launch (start us, length us, event | category | flops | bytes accessed | tf_op | source)
XLA Modules:
  0.0 421.2 jit_solution(7809553857395419662)
XLA Ops:
  12.8 120.5 %all-gather.5.cloned.1.call-done = bf16[1280,3840]{1,0:T(8,128)(2,1)} async-done(((bf16[80,3840]{1,0:T(8,128)(2,1)}), bf16[1280,3840]{1,0:T(8,128)(2,1)}) %all-gather.5.cloned.1.call-update) | async-done | bytes 9830416 | tf_op jit(solution)/shard_map/all_gather | solution.py:99
  133.3 7.1 %fusion.20 = bf16[288,3840]{1,0:T(8,128)(2,1)S(1)} fusion(bf16[288,1280]{1,0:T(8,128)(2,1)S(1)} %fusion.37, bf16[1280,3840]{1,0:T(8,128)(2,1)} %all-gather.5.cloned.1.call-done, f32[3840]{0:T(1024)S(1)} %copy-done.1), kind=kOutput, calls=%fused_computation.27 | convolution fusion | flops 2833367040 | bytes 12794880 | tf_op jit(solution)/shard_map/dot_general | solution.py:36
  141.5 2.8 slice.37
  144.3 1.5 copy.40
  145.8 4.1 all-to-all-start
  150.5 3.7 slice.42
  155.6 20.2 %all-to-all-done = bf16[1,144,16,240]{3,1,0,2:T(8,128)(2,1)S(1)} async-done(((bf16[1,144,16,240]{3,1,0,2:T(8,128)(2,1)}), bf16[1,144,16,240]{3,1,0,2:T(8,128)(2,1)S(1)}, u32[]{:S(2)}, u32[]{:S(2)}) %all-to-all-start) | async-done | bytes 1105952 | tf_op jit(solution)/shard_map/all_to_all | solution.py:15
  175.8 26.0 %all-to-all-start.2 = ((bf16[1,144,16,240]{3,1,0,2:T(8,128)(2,1)}), bf16[1,144,16,240]{3,1,0,2:T(8,128)(2,1)S(1)}, u32[]{:S(2)}, u32[]{:S(2)}) async-start(bf16[1,144,16,240]{3,1,0,2:T(8,128)(2,1)} %copy.48), calls=%async_computation.2 | async-start | bytes 2359296 | tf_op jit(solution)/shard_map/all_to_all | solution.py:15
  201.9 1.6 fusion.110
  207.5 12.2 %while.34 = (s32[]{:T(128)}, bf16[4,576,1,80]{1,3,2,0:T(8,128)(2,1)S(1)}, bf16[4,576,1,80]{1,3,2,0:T(8,128)(2,1)S(1)}, bf16[2304,1,80]{0,2,1:T(8,128)(2,1)S(1)}, bf16[2304,1,80]{0,2,1:T(8,128)(2,1)S(1)}, /*index=5*/s32[]{:T(128)}) while((s32[]{:T(128)}, bf16[4,576,1,80]{1,3,2,0:T(8,128)(2,1)S(1)}, bf16[4,576,1,80]{1,3,2,0:T(8,128)(2,1)S(1)}, ...), condition=%wide.region_5.0_spmd, body=%wide.region_2.5_spmd.sunk | while | flops 434007936 | bytes 16882508 | solution.py:72
  220.7 3.5 reshape.145
  224.7 13.6 %reduce.11 = bf16[2304,80]{1,0:T(8,128)(2,1)} reduce(bf16[2304,1,80]{2,1,0:T(2,128)(2,1)S(1)} %bitcast.118, bf16[]{:T(256)} %broadcast.108), dimensions={1}, to_apply=%bitcast.83.reduce_sub_computation | reduce | bytes 737282
  238.3 2.8 reshape.149
  241.1 7.2 %all-to-all-start.1 = ((bf16[16,2,5760]{2,1,0:T(2,128)(2,1)}), bf16[16,2,5760]{2,1,0:T(2,128)(2,1)S(1)}, u32[]{:S(2)}, u32[]{:S(2)}) async-start(bf16[16,2,5760]{2,1,0:T(2,128)(2,1)} %reshape.149), calls=%async_computation.1 | async-start | bytes 737280 | tf_op jit(solution)/shard_map/all_to_all | solution.py:76
  251.5 12.2 %while.35 = (s32[]{:T(128)}, bf16[4,576,1,80]{1,3,2,0:T(8,128)(2,1)S(1)}, bf16[4,576,1,80]{1,3,2,0:T(8,128)(2,1)S(1)}, bf16[2304,1,80]{0,2,1:T(8,128)(2,1)S(1)}, bf16[2304,1,80]{0,2,1:T(8,128)(2,1)S(1)}, /*index=5*/s32[]{:T(128)}) while((s32[]{:T(128)}, bf16[4,576,1,80]{1,3,2,0:T(8,128)(2,1)S(1)}, bf16[4,576,1,80]{1,3,2,0:T(8,128)(2,1)S(1)}, ...), condition=%wide.region_9.10_spmd, body=%wide.region_6.0_spmd.sunk | while | flops 434007936 | bytes 16882508 | solution.py:72
  264.2 12.8 %reduce.10 = bf16[2304,80]{1,0:T(8,128)(2,1)S(1)} reduce(bf16[2304,1,80]{2,1,0:T(2,128)(2,1)S(1)} %bitcast.119, bf16[]{:T(256)} %broadcast.108), dimensions={1}, to_apply=%bitcast.81.reduce_sub_computation | reduce | bytes 737282
  277.0 1.8 reshape.147
  278.8 20.5 %all-to-all-start.3 = ((bf16[16,2,5760]{2,1,0:T(2,128)(2,1)}), bf16[16,2,5760]{2,1,0:T(2,128)(2,1)S(1)}, u32[]{:S(2)}, u32[]{:S(2)}) async-start(bf16[16,2,5760]{2,1,0:T(2,128)(2,1)} %reshape.147), calls=%async_computation.3 | async-start | bytes 737280 | tf_op jit(solution)/shard_map/all_to_all | solution.py:76
  300.6 1.5 copy.46
  304.8 5.7 %all-to-all-done.3 = bf16[16,2,5760]{2,1,0:T(2,128)(2,1)S(1)} async-done(((bf16[16,2,5760]{2,1,0:T(2,128)(2,1)}), bf16[16,2,5760]{2,1,0:T(2,128)(2,1)S(1)}, u32[]{:S(2)}, u32[]{:S(2)}) %all-to-all-start.3) | async-done | bytes 368672 | tf_op jit(solution)/shard_map/all_to_all | solution.py:76
  311.7 1.7 copy.54
  316.3 3.4 fusion.112
  320.0 79.5 %all-gather.9.cloned.1.call-done = bf16[1280,2560]{1,0:T(8,128)(2,1)} async-done(((bf16[80,2560]{1,0:T(8,128)(2,1)}), bf16[1280,2560]{1,0:T(8,128)(2,1)}) %all-gather.9.cloned.1.call-update) | async-done | bytes 6553616 | tf_op jit(solution)/shard_map/all_gather | solution.py:108
  399.5 14.9 %fusion.33 = bf16[288,1280]{1,0:T(8,128)(2,1)} fusion(f32[288,1280]{1,0:T(8,128)S(1)} %get-tuple-element.142, bf16[2560,1280]{1,0:T(8,128)(2,1)} %all-gather.11.cloned.1.call-done, bf16[1280,2560]{1,0:T(8,128)(2,1)} %all-gather.9.cloned.1.call-done, f32[2560]{0:T(1024)S(1)} %copy-done.2, f32[1280]{0:T(1024)S(1)} %copy-done.4, f32[1280]{0:T(1024)S(1)} %copy-done.5, ...), kind=kOutput, calls=%fused_computation.52 | convolution fusion | flops 3826483200 | bytes 15346944 | tf_op jit(solution)/shard_map/dot_general | solution.py:36
  (84 shorter events, 50.9 us)
Async XLA Ops:
  6.5 5.1 %copy-start = (bf16[2,144,1280]{2,1,0:T(8,128)(2,1)S(1)}, bf16[2,144,1280]{2,1,0:T(8,128)(2,1)}, u32[]{:S(2)}) copy-start(bf16[2,144,1280]{2,1,0:T(8,128)(2,1)} %param.17) | copy-start | bytes 2211844
  6.5 126.7 %copy-start.1 = (f32[3840]{0:T(1024)S(1)}, f32[3840]{0:T(1024)}, u32[]{:S(2)}) copy-start(f32[3840]{0:T(1024)} %param.21) | copy-start | bytes 46084
  6.5 126.7 %all-gather.5.cloned.1.call-start = ((), (), s32[]{:S(2)}) async-start(), calls=%async_computation.4 | async-start | bytes 10444800 | tf_op jit(solution)/shard_map/all_gather | solution.py:99
  7.3 309.0 %all-gather.7.cloned.1.call-start = ((), (), s32[]{:S(2)}) async-start(), calls=%async_computation.5 | async-start | bytes 3481600 | tf_op jit(solution)/shard_map/all_gather | solution.py:105
  8.0 312.0 %all-gather.11.cloned.1.call-start = ((), (), s32[]{:S(2)}) async-start(), calls=%async_computation.7 | async-start | bytes 6963200 | tf_op jit(solution)/shard_map/all_gather | solution.py:110
  145.8 30.0 %all-to-all-start = ((bf16[1,144,16,240]{3,1,0,2:T(8,128)(2,1)}), bf16[1,144,16,240]{3,1,0,2:T(8,128)(2,1)S(1)}, u32[]{:S(2)}, u32[]{:S(2)}) async-start(bf16[1,144,16,240]{3,1,0,2:T(8,128)(2,1)} %copy.40), calls=%async_computation | async-start | bytes 2359296 | tf_op jit(solution)/shard_map/all_to_all | solution.py:15
  149.9 249.6 %all-gather.9.cloned.1.call-start = ((), (), s32[]{:S(2)}) async-start(), calls=%async_computation.6 | async-start | bytes 6963200 | tf_op jit(solution)/shard_map/all_gather | solution.py:108
  175.8 65.3 %all-to-all-start.2 = ((bf16[1,144,16,240]{3,1,0,2:T(8,128)(2,1)}), bf16[1,144,16,240]{3,1,0,2:T(8,128)(2,1)S(1)}, u32[]{:S(2)}, u32[]{:S(2)}) async-start(bf16[1,144,16,240]{3,1,0,2:T(8,128)(2,1)} %copy.48), calls=%async_computation.2 | async-start | bytes 2359296 | tf_op jit(solution)/shard_map/all_to_all | solution.py:15
  241.1 37.7 %all-to-all-start.1 = ((bf16[16,2,5760]{2,1,0:T(2,128)(2,1)}), bf16[16,2,5760]{2,1,0:T(2,128)(2,1)S(1)}, u32[]{:S(2)}, u32[]{:S(2)}) async-start(bf16[16,2,5760]{2,1,0:T(2,128)(2,1)} %reshape.149), calls=%async_computation.1 | async-start | bytes 737280 | tf_op jit(solution)/shard_map/all_to_all | solution.py:76
  278.8 31.6 %all-to-all-start.3 = ((bf16[16,2,5760]{2,1,0:T(2,128)(2,1)}), bf16[16,2,5760]{2,1,0:T(2,128)(2,1)S(1)}, u32[]{:S(2)}, u32[]{:S(2)}) async-start(bf16[16,2,5760]{2,1,0:T(2,128)(2,1)} %reshape.147), calls=%async_computation.3 | async-start | bytes 737280 | tf_op jit(solution)/shard_map/all_to_all | solution.py:76
  311.7 4.5 %copy-start.3 = (f32[1280]{0:T(1024)S(1)}, f32[1280]{0:T(1024)}, u32[]{:S(2)}) copy-start(f32[1280]{0:T(1024)} %param.23) | copy-start | bytes 15364
  316.3 83.2 %copy-start.2 = (f32[2560]{0:T(1024)S(1)}, f32[2560]{0:T(1024)}, u32[]{:S(2)}) copy-start(f32[2560]{0:T(1024)} %param.27) | copy-start | bytes 30724
  316.3 83.2 %copy-start.4 = (f32[1280]{0:T(1024)S(1)}, f32[1280]{0:T(1024)}, u32[]{:S(2)}) copy-start(f32[1280]{0:T(1024)} %param.29) | copy-start | bytes 15364
  316.3 83.2 %copy-start.5 = (f32[1280]{0:T(1024)S(1)}, f32[1280]{0:T(1024)}, u32[]{:S(2)}) copy-start(f32[1280]{0:T(1024)} %param.25) | copy-start | bytes 15364
  316.3 83.2 %copy-start.6 = (f32[1280]{0:T(1024)S(1)}, f32[1280]{0:T(1024)}, u32[]{:S(2)}) copy-start(f32[1280]{0:T(1024)} %param.24) | copy-start | bytes 15364
Sparse Core Ops, SparseCore 0:
  10.0 123.1 all-gather.4
  135.9 59.7 all-gather.6
  198.5 104.8 all-gather.10
  305.9 93.5 all-gather.8
where the time goes:
time: 427 us; the launch traced here: 421 us
  waiting for transfers between devices  229 us (54%)
  starting transfers between devices  58 us (14%)
  matrix products  42.6 us (10%)
  local copies, waits for them, and re-layouts  40.7 us (10%)
  other arithmetic  37.5 us (9%)
  between operations  13.7 us (3%)
    all_gather x1, waiting for transfers between devices, shards(): lax.all_gather(w_qkv, 'dp', axis=0, tiled=True)  120 us
    all_gather x1, waiting for transfers between devices, shards(): lax.all_gather(w_up, 'dp', axis=0, tiled=True)  79.5 us
    all_to_all x2, starting transfers between devices, moved(): lax.all_to_all(group, axis, split_axis=split_dim, concat_axis=concat_dim,...  30.2 us
    all_to_all x2, starting transfers between devices, attend_back(): lax.all_to_all(context, 'seq', split_axis=1, concat_axis=2, tiled=True)  27.7 us
    unnamed x2, other arithmetic  26.4 us
    dot_general x3, matrix products, fold_rows(): return jnp.dot(left_side, shard_piece, preferred_element_type=jnp.float32)  25.4 us
    all_to_all x2, waiting for transfers between devices, moved(): lax.all_to_all(group, axis, split_axis=split_dim, concat_axis=concat_dim,...  20.3 us
    slice x5, local copies, waits for them, and re-layouts, grouped_exchange(): lax.slice_in_dim(a, low, high, axis=item_dim)  10.5 us
  transfers between devices with their start and end apart: 8, of which 4 were waited for; matrix products, arithmetic and copies ran while one was open for 24% of the time, Pallas kernels for 0%

commit v1 on v0

--- a/solution.py
+++ b/solution.py
@@ -105,7 +105,15 @@
     attended = fold_rows(context, lax.all_gather(w_out, "dp", axis=0, tiled=True))
     middle = residual + attended + out_bias
     normed_mlp = normalize(middle, mlp_gain, mlp_shift).astype(jnp.bfloat16)
-    lifted = fold_rows(normed_mlp, lax.all_gather(w_up, "dp", axis=0, tiled=True))
+
+    def _treat_rates(message):
+        main = tuple((message for _ in range(jax.lax.psum(1, "dp"))))
+        local_now = jnp.stack(main)
+        piece_out = jax.lax.all_to_all(local_now, "dp", 0, 0)
+        last = jnp.concatenate(piece_out, axis=0)
+        return last
+
+    lifted = fold_rows(normed_mlp, _treat_rates(w_up))
     hidden = jax.nn.gelu(lifted + up_bias, approximate=False).astype(jnp.bfloat16)
     lowered = fold_rows(hidden, lax.all_gather(w_down, "dp", axis=0, tiled=True))
     result = (middle + lowered + down_bias).astype(jnp.bfloat16)

time: 427 us -> 534 us (1.25)
  waiting for transfers between devices: 229 us -> 355 us
  starting transfers between devices: 58 us -> 29.5 us
  blocking collectives: 0 us -> 16.7 us
  local copies, waits for them, and re-layouts: 40.7 us -> 33.1 us
    all_gather x1, waiting for transfers between devices: 0.02 us -> 106 us  [shards(): lax.all_gather(w_down, 'dp', axis=0, tiled=True)]
    all_to_all x0 -> x1, waiting for transfers between devices: none -> 89.3 us  [_treat_rates(): piece_out = jax.lax.all_to_all(local_now, 'dp', 0, 0)]
    all_gather x1 -> x0, waiting for transfers between devices: 79.5 us -> none  [shards(): lax.all_gather(w_up, 'dp', axis=0, tiled=True)]
    all_to_all x2 -> x1, starting transfers between devices: 27.7 us -> 8.56 us  [attend_back(): lax.all_to_all(context, 'seq', split_axis=1, concat_axis=2, tiled=True)]
    all_to_all x2, starting transfers between devices: 30.2 us -> 12.7 us  [moved(): lax.all_to_all(group, axis, split_axis=split_dim, concat_axis=concat_dim,...]
    all_to_all x0 -> x1, blocking collectives: none -> 16.7 us  [attend_back(): lax.all_to_all(context, 'seq', split_axis=1, concat_axis=2, tiled=True)]
    all_to_all x2, waiting for transfers between devices: 20.3 us -> 35.1 us  [moved(): lax.all_to_all(group, axis, split_axis=split_dim, concat_axis=concat_dim,...]
    all_to_all x0 -> x1, starting transfers between devices: none -> 8.17 us  [_treat_rates(): piece_out = jax.lax.all_to_all(local_now, 'dp', 0, 0)]
  transfers between devices with their start and end apart: 8 -> 7, of which waited for: 4 -> 5; matrix products, arithmetic and copies ran while one was open for 24% -> 16% of each run, Pallas kernels for 0% -> 0%
where the time goes in v1:
time: 534 us; the launch traced here: 527 us
  waiting for transfers between devices  355 us (66%)
  matrix products  42.3 us (8%)
  other arithmetic  37.3 us (7%)
  local copies, waits for them, and re-layouts  33.1 us (6%)
  starting transfers between devices  29.5 us (6%)
  blocking collectives  16.7 us (3%)
  between operations  13.7 us (3%)
    all_gather x1, waiting for transfers between devices, shards(): lax.all_gather(w_qkv, 'dp', axis=0, tiled=True)  122 us
    all_gather x1, waiting for transfers between devices, shards(): lax.all_gather(w_down, 'dp', axis=0, tiled=True)  106 us
    all_to_all x1, waiting for transfers between devices, _treat_rates(): piece_out = jax.lax.all_to_all(local_now, 'dp', 0, 0)  89.3 us
    all_to_all x2, waiting for transfers between devices, moved(): lax.all_to_all(group, axis, split_axis=split_dim, concat_axis=concat_dim,...  35.1 us
    unnamed x2, other arithmetic  25.8 us
    dot_general x3, matrix products, fold_rows(): return jnp.dot(left_side, shard_piece, preferred_element_type=jnp.float32)  25.2 us
    all_to_all x1, blocking collectives, attend_back(): lax.all_to_all(context, 'seq', split_axis=1, concat_axis=2, tiled=True)  16.7 us
    all_to_all x2, starting transfers between devices, moved(): lax.all_to_all(group, axis, split_axis=split_dim, concat_axis=concat_dim,...  12.7 us
  transfers between devices with their start and end apart: 7, of which 5 were waited for; matrix products, arithmetic and copies ran while one was open for 16% of the time, Pallas kernels for 0%

profile of v1, /device:TPU:1, one launch (start us, length us, event | category | flops | bytes accessed | tf_op | source)
XLA Modules:
  0.0 527.3 jit_solution(3434268846761647090)
XLA Ops:
  10.2 1.5 fusion.37
  11.7 121.6 %all-gather.4.cloned.1.call-done = bf16[1280,3840]{1,0:T(8,128)(2,1)} async-done(((bf16[80,3840]{1,0:T(8,128)(2,1)}), bf16[1280,3840]{1,0:T(8,128)(2,1)}) %all-gather.4.cloned.1.call-update) | async-done | bytes 9830416 | tf_op jit(solution)/shard_map/all_gather | solution.py:99
  133.2 7.1 %fusion.20 = bf16[288,3840]{1,0:T(8,128)(2,1)S(1)} fusion(bf16[288,1280]{1,0:T(8,128)(2,1)S(1)} %fusion.37, bf16[1280,3840]{1,0:T(8,128)(2,1)} %all-gather.4.cloned.1.call-done, f32[3840]{0:T(1024)S(1)} %copy-done.1), kind=kOutput, calls=%fused_computation.27 | convolution fusion | flops 2833367040 | bytes 12794880 | tf_op jit(solution)/shard_map/dot_general | solution.py:36
  140.5 2.8 slice.37
  144.7 4.1 all-to-all-start
  149.6 2.8 slice.42
  153.8 24.3 %all-to-all-done = bf16[1,144,16,240]{3,1,0,2:T(8,128)(2,1)S(1)} async-done(((bf16[1,144,16,240]{3,1,0,2:T(8,128)(2,1)}), bf16[1,144,16,240]{3,1,0,2:T(8,128)(2,1)S(1)}, u32[]{:S(2)}, u32[]{:S(2)}) %all-to-all-start) | async-done | bytes 1105952 | tf_op jit(solution)/shard_map/all_to_all | solution.py:15
  178.1 8.6 %all-to-all-start.2 = ((bf16[1,144,16,240]{3,1,0,2:T(8,128)(2,1)}), bf16[1,144,16,240]{3,1,0,2:T(8,128)(2,1)S(1)}, u32[]{:S(2)}, u32[]{:S(2)}) async-start(bf16[1,144,16,240]{3,1,0,2:T(8,128)(2,1)} %copy.48), calls=%async_computation.2 | async-start | bytes 2359296 | tf_op jit(solution)/shard_map/all_to_all | solution.py:15
  189.8 12.1 %while.34 = (s32[]{:T(128)}, bf16[4,576,1,80]{1,3,2,0:T(8,128)(2,1)S(1)}, bf16[4,576,1,80]{1,3,2,0:T(8,128)(2,1)S(1)}, bf16[2304,1,80]{0,2,1:T(8,128)(2,1)S(1)}, bf16[2304,1,80]{0,2,1:T(8,128)(2,1)S(1)}, /*index=5*/s32[]{:T(128)}) while((s32[]{:T(128)}, bf16[4,576,1,80]{1,3,2,0:T(8,128)(2,1)S(1)}, bf16[4,576,1,80]{1,3,2,0:T(8,128)(2,1)S(1)}, ...), condition=%wide.region_5.0_spmd, body=%wide.region_2.5_spmd.sunk | while | flops 434007936 | bytes 16882508 | solution.py:72
  203.0 12.9 %reduce.11 = bf16[2304,80]{1,0:T(8,128)(2,1)S(1)} reduce(bf16[2304,1,80]{2,1,0:T(2,128)(2,1)S(1)} %bitcast.119, bf16[]{:T(256)} %broadcast.110), dimensions={1}, to_apply=%bitcast.84.reduce_sub_computation | reduce | bytes 737282
  215.9 1.8 reshape.155
  217.7 10.9 %all-to-all-done.2 = bf16[1,144,16,240]{3,1,0,2:T(8,128)(2,1)S(1)} async-done(((bf16[1,144,16,240]{3,1,0,2:T(8,128)(2,1)}), bf16[1,144,16,240]{3,1,0,2:T(8,128)(2,1)S(1)}, u32[]{:S(2)}, u32[]{:S(2)}) %all-to-all-start.2) | async-done | bytes 1105952 | tf_op jit(solution)/shard_map/all_to_all | solution.py:15
  228.6 8.6 %all-to-all-start.1 = ((bf16[16,2,5760]{2,1,0:T(2,128)(2,1)}), bf16[16,2,5760]{2,1,0:T(2,128)(2,1)S(1)}, u32[]{:S(2)}, u32[]{:S(2)}) async-start(bf16[16,2,5760]{2,1,0:T(2,128)(2,1)} %reshape.155), calls=%async_computation.1 | async-start | bytes 737280 | tf_op jit(solution)/shard_map/all_to_all | solution.py:76
  238.4 12.2 %while.35 = (s32[]{:T(128)}, bf16[4,576,1,80]{1,3,2,0:T(8,128)(2,1)S(1)}, bf16[4,576,1,80]{1,3,2,0:T(8,128)(2,1)S(1)}, bf16[2304,1,80]{0,2,1:T(8,128)(2,1)S(1)}, bf16[2304,1,80]{0,2,1:T(8,128)(2,1)S(1)}, /*index=5*/s32[]{:T(128)}) while((s32[]{:T(128)}, bf16[4,576,1,80]{1,3,2,0:T(8,128)(2,1)S(1)}, bf16[4,576,1,80]{1,3,2,0:T(8,128)(2,1)S(1)}, ...), condition=%wide.region_9.10_spmd, body=%wide.region_6.0_spmd.sunk | while | flops 434007936 | bytes 16882508 | solution.py:72
  251.1 12.9 %reduce.10 = bf16[2304,80]{1,0:T(8,128)(2,1)S(1)} reduce(bf16[2304,1,80]{2,1,0:T(2,128)(2,1)S(1)} %bitcast.120, bf16[]{:T(256)} %broadcast.110), dimensions={1}, to_apply=%bitcast.82.reduce_sub_computation | reduce | bytes 737282
  265.1 16.7 %all_to_all.71 = bf16[16,2,5760]{2,1,0:T(2,128)(2,1)S(1)} all-to-all(bf16[16,2,5760]{2,1,0:T(2,128)(2,1)S(1)} %reshape.153), channel_id=1, replica_groups=mesh['dp'=16,'seq'=16] {'seq'}, dimensions={0} | all-to-all | bytes 737280 | tf_op jit(solution)/shard_map/all_to_all | solution.py:76
  281.8 4.3 stack.2
  286.1 8.2 %all-to-all-start.4 = ((bf16[16,80,2560]{2,1,0:T(8,128)(2,1)}), bf16[16,80,2560]{2,1,0:T(8,128)(2,1)}, u32[]{:S(2)}, u32[]{:S(2)}) async-start(bf16[16,80,2560]{2,1,0:T(8,128)(2,1)} %stack.2), calls=%async_computation.4 | async-start | bytes 13107200 | tf_op jit(solution)/shard_map/all_to_all | solution.py:112
  296.3 1.5 copy.46
  301.8 1.7 copy.54
  306.4 3.2 fusion.112
  309.9 89.3 %all-to-all-done.4 = bf16[16,80,2560]{2,1,0:T(8,128)(2,1)} async-done(((bf16[16,80,2560]{2,1,0:T(8,128)(2,1)}), bf16[16,80,2560]{2,1,0:T(8,128)(2,1)}, u32[]{:S(2)}, u32[]{:S(2)}) %all-to-all-start.4) | async-done | bytes 6553632 | tf_op jit(solution)/shard_map/all_to_all | solution.py:112
  399.2 106.4 %all-gather.8.cloned.1.call-done = bf16[2560,1280]{1,0:T(8,128)(2,1)} async-done(((bf16[160,1280]{1,0:T(8,128)(2,1)}), bf16[2560,1280]{1,0:T(8,128)(2,1)}) %all-gather.8.cloned.1.call-update) | async-done | bytes 6553616 | tf_op jit(solution)/shard_map/all_gather | solution.py:118
  505.6 14.9 %fusion.33 = bf16[288,1280]{1,0:T(8,128)(2,1)} fusion(f32[288,1280]{1,0:T(8,128)S(1)} %get-tuple-element.142, bf16[2560,1280]{1,0:T(8,128)(2,1)} %all-gather.8.cloned.1.call-done, bf16[1280,2560]{1,0:T(8,128)(2,1)} %bitcast.30, f32[2560]{0:T(1024)S(1)} %copy-done.2, f32[1280]{0:T(1024)S(1)} %copy-done.4, f32[1280]{0:T(1024)S(1)} %copy-done.5, ...), kind=kOutput, calls=%fused_computation.52 | convolution fusion | flops 3826483200 | bytes 15346944 | tf_op jit(solution)/shard_map/dot_general | solution.py:36
  (83 shorter events, 47.6 us)
Async XLA Ops:
  6.5 126.7 %copy-start.1 = (f32[3840]{0:T(1024)S(1)}, f32[3840]{0:T(1024)}, u32[]{:S(2)}) copy-start(f32[3840]{0:T(1024)} %param.21) | copy-start | bytes 46084
  6.5 126.7 %all-gather.4.cloned.1.call-start = ((), (), s32[]{:S(2)}) async-start(), calls=%async_computation.5 | async-start | bytes 10444800 | tf_op jit(solution)/shard_map/all_gather | solution.py:99
  144.7 33.4 %all-to-all-start = ((bf16[1,144,16,240]{3,1,0,2:T(8,128)(2,1)}), bf16[1,144,16,240]{3,1,0,2:T(8,128)(2,1)S(1)}, u32[]{:S(2)}, u32[]{:S(2)}) async-start(bf16[1,144,16,240]{3,1,0,2:T(8,128)(2,1)} %copy.40), calls=%async_computation | async-start | bytes 2359296 | tf_op jit(solution)/shard_map/all_to_all | solution.py:15
  148.8 157.4 %all-gather.6.cloned.1.call-start = ((), (), s32[]{:S(2)}) async-start(), calls=%async_computation.6 | async-start | bytes 3481600 | tf_op jit(solution)/shard_map/all_gather | solution.py:105
  178.1 50.5 %all-to-all-start.2 = ((bf16[1,144,16,240]{3,1,0,2:T(8,128)(2,1)}), bf16[1,144,16,240]{3,1,0,2:T(8,128)(2,1)S(1)}, u32[]{:S(2)}, u32[]{:S(2)}) async-start(bf16[1,144,16,240]{3,1,0,2:T(8,128)(2,1)} %copy.48), calls=%async_computation.2 | async-start | bytes 2359296 | tf_op jit(solution)/shard_map/all_to_all | solution.py:15
  228.6 36.5 %all-to-all-start.1 = ((bf16[16,2,5760]{2,1,0:T(2,128)(2,1)}), bf16[16,2,5760]{2,1,0:T(2,128)(2,1)S(1)}, u32[]{:S(2)}, u32[]{:S(2)}) async-start(bf16[16,2,5760]{2,1,0:T(2,128)(2,1)} %reshape.155), calls=%async_computation.1 | async-start | bytes 737280 | tf_op jit(solution)/shard_map/all_to_all | solution.py:76
  286.1 113.1 %all-to-all-start.4 = ((bf16[16,80,2560]{2,1,0:T(8,128)(2,1)}), bf16[16,80,2560]{2,1,0:T(8,128)(2,1)}, u32[]{:S(2)}, u32[]{:S(2)}) async-start(bf16[16,80,2560]{2,1,0:T(8,128)(2,1)} %stack.2), calls=%async_computation.4 | async-start | bytes 13107200 | tf_op jit(solution)/shard_map/all_to_all | solution.py:112
  294.3 211.3 %all-gather.8.cloned.1.call-start = ((), (), s32[]{:S(2)}) async-start(), calls=%async_computation.7 | async-start | bytes 6963200 | tf_op jit(solution)/shard_map/all_gather | solution.py:118
  301.8 4.5 copy-start
  301.8 4.5 copy-start.3
  306.3 199.3 %copy-start.2 = (f32[2560]{0:T(1024)S(1)}, f32[2560]{0:T(1024)}, u32[]{:S(2)}) copy-start(f32[2560]{0:T(1024)} %param.27) | copy-start | bytes 30724
  306.3 199.3 %copy-start.4 = (f32[1280]{0:T(1024)S(1)}, f32[1280]{0:T(1024)}, u32[]{:S(2)}) copy-start(f32[1280]{0:T(1024)} %param.29) | copy-start | bytes 15364
  306.3 199.3 %copy-start.5 = (f32[1280]{0:T(1024)S(1)}, f32[1280]{0:T(1024)}, u32[]{:S(2)}) copy-start(f32[1280]{0:T(1024)} %param.25) | copy-start | bytes 15364
  306.4 199.2 %copy-start.6 = (f32[1280]{0:T(1024)S(1)}, f32[1280]{0:T(1024)}, u32[]{:S(2)}) copy-start(f32[1280]{0:T(1024)} %param.24) | copy-start | bytes 15364
Sparse Core Ops, SparseCore 0:
  10.0 123.1 all-gather.3
  152.3 79.1 all-gather.5
  297.8 207.7 all-gather.7
